TPU v7x, 32 devices: a whole 2x2x4 slice. The times are simulated.
32 devices in a mesh: dp: 2 (over x), ctx: 4 (over y, core), tp: 4 (over z).
Axes of the slice: x: 2, y: 2, z: 4, core: 2. Of those that a mesh axis runs over, the one named last changes fastest.
Arguments:
- layer_input: bfloat16 [2, 1024, 8192], P('dp', ('ctx', 'tp')), may hold values from -6 to 6
- value_weight: bfloat16 [8192, 1024], P(('dp', 'ctx'), 'tp'), may hold values from -0.0625 to 0.0625
- query_raw: bfloat16 [2, 1024, 1024], P('dp', 'ctx', 'tp'), may hold values from -6 to 6
- key_raw: bfloat16 [2, 1024, 1024], P('dp', 'ctx', 'tp'), may hold values from -6 to 6
- out_grad: bfloat16 [2, 1024, 1024], P('dp', 'ctx', 'tp'), may hold values from -6 to 6
- gate_logits: float32 [2, 2, 8, 1024], P(None, 'dp', 'tp', 'ctx'), may hold values from -14 to 4, as said below
- decay_params: float32 [2, 8], P(None, 'tp'), may hold values from -0.35 to 0.35
- saved_states: float32 [2, 4, 8, 128, 128], P('dp', 'ctx', 'tp'), may hold values from -4 to 4
Outputs:
- input_grad: bfloat16 [2, 1024, 8192], P('dp', ('ctx', 'tp'))
- query_grad: bfloat16 [2, 1024, 1024], P('dp', 'ctx', 'tp')
- key_grad: bfloat16 [2, 1024, 1024], P('dp', 'ctx', 'tp')
- gate_grad: float32 [2, 2, 8, 1024], P(None, 'dp', 'tp', 'ctx')
- decay_grad: float32 [2, 8], P(None, 'tp')
Inputs may be any that keep to these rules, and one draw needn't show every extreme that they name: `gate_logits`: row 0 holds decay logits, row 1 write-strength logits.
All inputs are finite; a program needn't handle non-finite values.
Results may differ from a plain program's by a relative error of at most 0.015.
Values may be sent and summed in bfloat16 or wider, within the bound.
A program may use at most 64 MiB of HBM per device.

v0:
```python
import jax
import jax.numpy as jnp
from jax import lax
from jax.sharding import PartitionSpec as P

SUBLEN = 64


epsilon = 1e-06
highest = lax.Precision.HIGHEST


def entering(shard, axis, combine, identity):
    size, place = (lax.axis_size(axis), lax.axis_index(axis))
    everything = jax.tree.map(
        lambda part, kind: lax.all_gather(part.astype(kind), axis),
        shard,
        jax.tree.map(lambda a: jnp.bfloat16 if a.dtype == jnp.float32 else a.dtype, shard),
    )
    start = jax.tree.map(
        lambda part, zero: jnp.broadcast_to(jnp.asarray(zero, part.dtype), part.shape),
        shard,
        identity,
    )

    def turn(k, before):
        at = size - 1 - k
        reached = at > place
        new = combine(
            before, jax.tree.map(lambda part, own: part[at].astype(own.dtype), everything, shard)
        )
        return jax.tree.map(lambda a, b: jnp.where(reached, a, b), new, before)

    return lax.fori_loop(0, size, turn, start)


def inner_step(carried, pieces):
    query_unit, key_unit, values, log_decay, strengths = pieces
    sub_len = query_unit.shape[0]
    head_dim = query_unit.shape[1]
    cumulative = jnp.cumsum(log_decay)
    positions = jnp.arange(sub_len)
    lower_mask = positions[:, None] >= positions[None, :]
    strict_mask = positions[:, None] > positions[None, :]
    spread = jnp.where(lower_mask, cumulative[:, None] - cumulative[None, :], 0.0)
    decays = jnp.where(lower_mask, jnp.exp(spread), 0.0)
    key_gram = jnp.dot(key_unit, key_unit.T, precision=highest)
    system = jnp.eye(sub_len, dtype=jnp.float32) + jnp.where(
        strict_mask, strengths[:, None] * decays * key_gram, 0.0
    )
    right_side = jnp.concatenate(
        [(strengths * jnp.exp(cumulative))[:, None] * key_unit, strengths[:, None] * values], axis=1
    )
    solved = jax.scipy.linalg.solve_triangular(system, right_side, lower=True, unit_diagonal=True)
    new_values = solved[:, head_dim:] - jnp.dot(solved[:, :head_dim], carried, precision=highest)
    scores = decays * jnp.dot(query_unit, key_unit.T, precision=highest)
    output = jnp.dot(
        query_unit * jnp.exp(cumulative)[:, None], carried, precision=highest
    ) + jnp.dot(scores, new_values, precision=highest)
    tail_decay = jnp.exp(cumulative[-1] - cumulative)
    updated = jnp.exp(cumulative[-1]) * carried + jnp.dot(
        (key_unit * tail_decay[:, None]).T, new_values, precision=highest
    )
    return (updated, output)


def core(query_row, key_row, values, gate_a, gate_b, params, initial):
    length = query_row.shape[0]
    head_dim = query_row.shape[1]
    query_unit = (
        query_row
        * lax.rsqrt(jnp.sum(query_row * query_row, axis=-1, keepdims=True) + epsilon)
        * head_dim ** (-0.5)
    )
    key_unit = key_row * lax.rsqrt(jnp.sum(key_row * key_row, axis=-1, keepdims=True) + epsilon)
    log_decay = -jnp.exp(params[0]) * jax.nn.softplus(gate_a + params[1])
    strengths = jax.nn.sigmoid(gate_b)
    blocks = length // SUBLEN

    def into_blocks(array):
        return array.reshape((blocks, SUBLEN) + array.shape[1:])

    final_state, outputs = lax.scan(
        inner_step,
        initial,
        (
            into_blocks(query_unit),
            into_blocks(key_unit),
            into_blocks(values),
            into_blocks(log_decay),
            into_blocks(strengths),
        ),
    )
    return (outputs.reshape(length, head_dim), final_state)


def core_heads(query_rows, key_rows, values, gate_a, gate_b, params, initial):
    mapped = jax.vmap(core, in_axes=(0, 0, 0, 0, 0, 1, 0))
    return mapped(query_rows, key_rows, values, gate_a, gate_b, params, initial)


def compose(early_map, late_map):
    matrix = jnp.einsum("hij,hjk->hik", late_map[0], early_map[0], precision=highest)
    offset_part = (
        jnp.einsum("hij,hjk->hik", late_map[0], early_map[1], precision=highest) + late_map[1]
    )
    return (matrix, offset_part)


def per_device(
    layer_input, value_weight, query_raw, key_raw, out_grad, gate_logits, decay_params, saved_states
):
    tokens_all = lax.all_gather(layer_input, "tp", axis=1, tiled=True)[0]
    length = tokens_all.shape[0]
    head_dim = saved_states.shape[-1]
    head_count = query_raw.shape[2] // head_dim
    weight_full = lax.all_gather(value_weight, ("dp", "ctx"), axis=0, tiled=True)
    value_flat = jnp.dot(tokens_all, weight_full, preferred_element_type=jnp.float32)
    value_round = value_flat.astype(jnp.bfloat16)

    def split_heads(flat_rows):
        return (
            flat_rows.reshape(length, head_count, head_dim).transpose(1, 0, 2).astype(jnp.float32)
        )

    query_heads = split_heads(query_raw[0])
    key_heads = split_heads(key_raw[0])
    value_heads = split_heads(value_round)
    decay_logit = gate_logits[0, 0]
    strength_logit = gate_logits[1, 0]
    initial_states = saved_states[0, 0]
    outputs, pullback = jax.vjp(
        core_heads,
        query_heads,
        key_heads,
        value_heads,
        decay_logit,
        strength_logit,
        decay_params,
        initial_states,
    )
    cotangent = split_heads(out_grad[0])
    zeros_state = jnp.zeros_like(initial_states)
    identity_states = jnp.broadcast_to(jnp.eye(head_dim, dtype=jnp.float32), initial_states.shape)
    transition = core_heads(
        query_heads,
        key_heads,
        jnp.zeros_like(value_heads),
        decay_logit,
        strength_logit,
        decay_params,
        identity_states,
    )[1]
    local_part = pullback((cotangent, zeros_state))[6]
    affine_maps = (jnp.swapaxes(transition, 1, 2), local_part)
    incoming = entering(affine_maps, "ctx", compose, (identity_states, zeros_state))[1]
    gradients = pullback((cotangent, incoming))
    query_grad = (
        gradients[0]
        .transpose(1, 0, 2)
        .reshape(length, head_count * head_dim)
        .astype(jnp.bfloat16)[None]
    )
    key_grad = (
        gradients[1]
        .transpose(1, 0, 2)
        .reshape(length, head_count * head_dim)
        .astype(jnp.bfloat16)[None]
    )
    value_grad = (
        gradients[2].transpose(1, 0, 2).reshape(length, head_count * head_dim).astype(jnp.bfloat16)
    )
    gate_grad = jnp.stack([gradients[3], gradients[4]])[:, None]
    decay_grad = lax.psum(gradients[5], ("dp", "ctx"))
    summed = lax.psum_scatter(
        lax.dot_general(
            value_grad, weight_full, (((1,), (1,)), ((), ())), preferred_element_type=jnp.float32
        ).astype(jnp.bfloat16),
        "tp",
        scatter_dimension=0,
        tiled=True,
    )
    input_grad = summed[None]
    return (input_grad, query_grad, key_grad, gate_grad, decay_grad)


def solution(mesh):
    placed = (
        P("dp", ("ctx", "tp"), None),
        P(("dp", "ctx"), "tp"),
        P("dp", "ctx", "tp"),
        P("dp", "ctx", "tp"),
        P("dp", "ctx", "tp"),
        P(None, "dp", "tp", "ctx"),
        P(None, "tp"),
        P("dp", "ctx", "tp", None, None),
    )
    return jax.shard_map(
        per_device,
        mesh=mesh,
        in_specs=placed,
        out_specs=(
            P("dp", ("ctx", "tp"), None),
            P("dp", "ctx", "tp"),
            P("dp", "ctx", "tp"),
            P(None, "dp", "tp", "ctx"),
            P(None, "tp"),
        ),
        check_vma=False,
    )
```

profile of v0, /device:TPU:9, one launch (start us, length us, event | category | flops | bytes accessed | tf_op | source)
XLA Modules:
  0.0 467.1 jit_solution(16357434272894257928)
XLA Ops:
  15.9 53.4 %while.131 = (s32[]{:T(128)}, f32[2,128,128]{2,1,0:T(8,128)S(1)}, f32[4,2,64]{2,1,0:T(2,128)}, f32[4,2,64,128]{3,2,1,0:T(8,128)S(1)}, f32[4,2,64]{2,1,0:T(2,128)}, /*index=5*/s32[]{:T(128)}, f32[]{:T(128)}) while((s32[]{:T(128)}, f32[2,128,128]{2,1,0:T(8,128)S(1)}, f32[4,2,64]{2,1,0:T(2,128)}, f32[4,2,64,128]{3,2,1,0:T(8,128)S(1)}, ...), condition=%wide.region_3.5_spmd, body=%wide.region_1.4_spmd.sunk | while | flops 88338752 | bytes 1457805 | solution.py:83
  18.1 9.8 %custom-call.48 = f32[2,1,64,64]{2,3,1,0:T(8,128)S(1)} custom-call(f32[2,1,64,64]{3,2,1,0:T(8,128)S(1)} %fusion.305), custom_call_target="InvertDiagBlocksLowerTriangular" | custom-call | tf_op jit(solution)/shard_map/vmap()/while/body/eval_jaxpr/jit(_solve_triangular)/triangular_solve/custom-call.1 | solution.py:54
  31.5 9.8 %custom-call.48 = f32[2,1,64,64]{2,3,1,0:T(8,128)S(1)} custom-call(f32[2,1,64,64]{3,2,1,0:T(8,128)S(1)} %fusion.305), custom_call_target="InvertDiagBlocksLowerTriangular" | custom-call | tf_op jit(solution)/shard_map/vmap()/while/body/eval_jaxpr/jit(_solve_triangular)/triangular_solve/custom-call.1 | solution.py:54
  44.8 9.8 %custom-call.48 = f32[2,1,64,64]{2,3,1,0:T(8,128)S(1)} custom-call(f32[2,1,64,64]{3,2,1,0:T(8,128)S(1)} %fusion.305), custom_call_target="InvertDiagBlocksLowerTriangular" | custom-call | tf_op jit(solution)/shard_map/vmap()/while/body/eval_jaxpr/jit(_solve_triangular)/triangular_solve/custom-call.1 | solution.py:54
  58.1 9.8 %custom-call.48 = f32[2,1,64,64]{2,3,1,0:T(8,128)S(1)} custom-call(f32[2,1,64,64]{3,2,1,0:T(8,128)S(1)} %fusion.305), custom_call_target="InvertDiagBlocksLowerTriangular" | custom-call | tf_op jit(solution)/shard_map/vmap()/while/body/eval_jaxpr/jit(_solve_triangular)/triangular_solve/custom-call.1 | solution.py:54
  69.4 6.7 %all-gather = bf16[8,128,128]{2,1,0:T(8,128)(2,1)} all-gather(bf16[2,128,128]{2,1,0:T(8,128)(2,1)S(1)} %bitcast.638), channel_id=2, replica_groups=mesh['dp'=2,'ctx'=4,'tp'=4] {'ctx'}, dimensions={0}, use_global_device_ids=true | all-gather | bytes 327680 | tf_op jit(solution)/shard_map/all_gather | solution.py:16
  77.5 11.4 %all-gather.5.cloned.1.call-done = bf16[1,256,8192]{2,1,0:T(8,128)(2,1)} async-done(((bf16[1,64,8192]{2,1,0:T(8,128)(2,1)}), bf16[1,256,8192]{2,1,0:T(8,128)(2,1)}) %all-gather.5.cloned.1.call-update) | async-done | bytes 4194320 | tf_op jit(solution)/shard_map/all_gather | solution.py:113
  88.9 40.1 %all-gather.7.cloned.1.call-done = bf16[8192,256]{1,0:T(8,128)(2,1)} async-done(((bf16[1024,256]{1,0:T(8,128)(2,1)}), bf16[8192,256]{1,0:T(8,128)(2,1)}) %all-gather.7.cloned.1.call-update) | async-done | bytes 4194320 | tf_op jit(solution)/shard_map/all_gather | solution.py:117
  129.0 5.2 %fusion.188 = bf16[256,256]{0,1:T(8,128)(2,1)S(1)} fusion(bf16[8192,256]{1,0:T(8,128)(2,1)} %all-gather.7.cloned.1.call-done, bf16[1,256,8192]{2,1,0:T(8,128)(2,1)} %all-gather.5.cloned.1.call-done), kind=kOutput, calls=%fused_computation.289 | convolution fusion | flops 1073807360 | bytes 8519680 | tf_op jit(solution)/shard_map/dot_general | solution.py:118
  137.1 91.0 %while.132 = (s32[]{:T(128)}, f32[2,128,128]{2,1,0:T(8,128)S(1)}, f32[4,2,64,64]{3,2,1,0:T(8,128)}, f32[4,2,128,64]{2,3,1,0:T(8,128)S(1)}, f32[4,2,64,64]{3,2,1,...) while((s32[]{:T(128)}, f32[2,128,128]{2,1,0:T(8,128)S(1)}, ...), condition=%wide.region_7.9_spmd.clone.clone, body=%wide.region_5.8_spmd.clone.clone.sunk | while | flops 101061184 | bytes 3349921 | solution.py:83
  141.6 10.6 %custom-call.49 = f32[2,1,64,64]{2,3,1,0:T(8,128)S(1)} custom-call(f32[2,1,64,64]{3,2,1,0:T(8,128)} %get-tuple-element.3131), custom_call_target="InvertDiagBlocksLowerTriangular" | custom-call | tf_op jit(solution)/shard_map/jvp(vmap())/while/body/eval_jaxpr/jit(_solve_triangular)/triangular_solve/custom-call.1 | solution.py:54
  156.3 1.3 constant_dynamic-update-slice_fusion.15
  164.4 10.6 %custom-call.49 = f32[2,1,64,64]{2,3,1,0:T(8,128)S(1)} custom-call(f32[2,1,64,64]{3,2,1,0:T(8,128)} %get-tuple-element.3131), custom_call_target="InvertDiagBlocksLowerTriangular" | custom-call | tf_op jit(solution)/shard_map/jvp(vmap())/while/body/eval_jaxpr/jit(_solve_triangular)/triangular_solve/custom-call.1 | solution.py:54
  179.1 1.3 constant_dynamic-update-slice_fusion.15
  187.1 10.6 %custom-call.49 = f32[2,1,64,64]{2,3,1,0:T(8,128)S(1)} custom-call(f32[2,1,64,64]{3,2,1,0:T(8,128)} %get-tuple-element.3131), custom_call_target="InvertDiagBlocksLowerTriangular" | custom-call | tf_op jit(solution)/shard_map/jvp(vmap())/while/body/eval_jaxpr/jit(_solve_triangular)/triangular_solve/custom-call.1 | solution.py:54
  201.8 1.3 constant_dynamic-update-slice_fusion.15
  209.9 10.6 %custom-call.49 = f32[2,1,64,64]{2,3,1,0:T(8,128)S(1)} custom-call(f32[2,1,64,64]{3,2,1,0:T(8,128)} %get-tuple-element.3131), custom_call_target="InvertDiagBlocksLowerTriangular" | custom-call | tf_op jit(solution)/shard_map/jvp(vmap())/while/body/eval_jaxpr/jit(_solve_triangular)/triangular_solve/custom-call.1 | solution.py:54
  224.5 1.3 constant_dynamic-update-slice_fusion.15
  228.1 21.0 %while.134 = (s32[]{:T(128)}, f32[2,128,128]{2,1,0:T(8,128)S(1)}, f32[4,2,1,1]{1,3,2,0:T(1,128)}, f32[4,2,64,128]{3,2,1,0:T(8,128)}, f32[4,2,64,128]{3,2,1,0:T(8...) while((s32[]{:T(128)}, f32[2,128,128]{2,1,0:T(8,128)S(1)}, ...), condition=%wide.region_9.11_spmd.clone, body=%wide.region_8.10_spmd.clone.sunk | while | flops 88276992 | bytes 1313951 | solution.py:83
  249.1 6.5 %all-gather.1 = bf16[8,128,128]{2,1,0:T(8,128)(2,1)} all-gather(bf16[2,128,128]{2,1,0:T(8,128)(2,1)S(1)} %convert_element_type.145), channel_id=3, replica_groups=mesh['dp'=2,'ctx'=4,'tp'=4] {'ctx'}, dimensions={0}, use_global_device_ids=true | all-gather | bytes 327680 | tf_op jit(solution)/shard_map/all_gather | solution.py:16
  255.6 4.6 while.135
  261.7 115.9 %while.133 = (s32[]{:T(128)}, f32[2,128,128]{2,1,0:T(8,128)S(1)}, f32[4,2,64,128]{3,2,0,1:T(8,128)}, f32[4,2,64,128]{3,2,0,1:T(8,128)}, bf16[4,2,64,128]{3,2,0,1...) while((s32[]{:T(128)}, f32[2,128,128]{2,1,0:T(8,128)S(1)}, ...), condition=%wide.region_23.25_spmd.clone.clone, body=%wide.region_12.24_spmd.clone.clone.sunk | while | flops 283858112 | bytes 5431853 | solution.py:83
  266.5 9.8 %custom-call.50 = f32[2,1,64,64]{2,3,1,0:T(8,128)S(1)} custom-call(f32[2,1,64,64]{3,2,1,0:T(8,128)S(1)} %add_bitcast_fusion.3), custom_call_target="InvertDiagBlocksLowerTriangular" | custom-call | tf_op jit(solution)/shard_map/transpose(jvp(vmap()))/while/body/eval_jaxpr/jit(_solve_triangular)/triangular_solve | solution.py:54
  277.0 1.2 fusion.346
  295.6 9.8 %custom-call.50 = f32[2,1,64,64]{2,3,1,0:T(8,128)S(1)} custom-call(f32[2,1,64,64]{3,2,1,0:T(8,128)S(1)} %add_bitcast_fusion.3), custom_call_target="InvertDiagBlocksLowerTriangular" | custom-call | tf_op jit(solution)/shard_map/transpose(jvp(vmap()))/while/body/eval_jaxpr/jit(_solve_triangular)/triangular_solve | solution.py:54
  306.1 1.2 fusion.346
  324.6 9.8 %custom-call.50 = f32[2,1,64,64]{2,3,1,0:T(8,128)S(1)} custom-call(f32[2,1,64,64]{3,2,1,0:T(8,128)S(1)} %add_bitcast_fusion.3), custom_call_target="InvertDiagBlocksLowerTriangular" | custom-call | tf_op jit(solution)/shard_map/transpose(jvp(vmap()))/while/body/eval_jaxpr/jit(_solve_triangular)/triangular_solve | solution.py:54
  353.5 9.8 %custom-call.50 = f32[2,1,64,64]{2,3,1,0:T(8,128)S(1)} custom-call(f32[2,1,64,64]{3,2,1,0:T(8,128)S(1)} %add_bitcast_fusion.3), custom_call_target="InvertDiagBlocksLowerTriangular" | custom-call | tf_op jit(solution)/shard_map/transpose(jvp(vmap()))/while/body/eval_jaxpr/jit(_solve_triangular)/triangular_solve | solution.py:54
  363.9 1.2 fusion.346
  378.6 5.5 %convolution_convert_fusion = bf16[256,8192]{1,0:T(8,128)(2,1)} fusion(bf16[256,256]{0,1:T(8,128)(2,1)S(1)} %bitcast.633, bf16[8192,256]{1,0:T(8,128)(2,1)} %all-gather.7.cloned.1.call-done), kind=kOutput, calls=%fused_computation.286 | convolution fusion | flops 1075838976 | bytes 8519680 | tf_op jit(solution)/shard_map/dot_general | solution.py:176
  385.0 11.9 %psum.7 = f32[2,2]{1,0:T(2,128)} all-reduce(f32[2,2]{1,0:T(2,128)S(1)} %pad_add_fusion.3), channel_id=1, replica_groups=mesh['dp'=2,'ctx'=4,'tp'=4] {'dp','ctx'}, use_global_device_ids=true, to_apply=%region_29.31 | all-reduce | flops 4 | bytes 32 | tf_op jit(solution)/shard_map/psum | solution.py:174
  399.9 60.6 %reduce-scatter.2.cloned.1.call-done = bf16[64,8192]{1,0:T(8,128)(2,1)} async-done(((bf16[256,8192]{1,0:T(8,128)(2,1)}), bf16[64,8192]{1,0:T(8,128)(2,1)}) %reduce-scatter.2.cloned.1.call-update) | async-done | bytes 1048592 | tf_op jit(solution)/shard_map/reduce_scatter | solution.py:175
  (459 shorter events, 173.4 us)
Async XLA Ops:
  7.2 6.0 %copy-start.4 = (bf16[1,256,256]{2,1,0:T(8,128)(2,1)S(1)}, bf16[1,256,256]{2,1,0:T(8,128)(2,1)}, u32[]{:S(2)}) copy-start(bf16[1,256,256]{2,1,0:T(8,128)(2,1)} %param.24) | copy-start | bytes 393220
  7.2 81.7 %all-gather.5.cloned.1.call-start = ((), (), s32[]{:S(2)}) async-start(), calls=%async_computation.1 | async-start | bytes 5242880 | tf_op jit(solution)/shard_map/all_gather | solution.py:113
  7.9 121.1 %all-gather.7.cloned.1.call-start = ((), (), s32[]{:S(2)}) async-start(), calls=%async_computation.2 | async-start | bytes 4718592 | tf_op jit(solution)/shard_map/all_gather | solution.py:117
  8.7 451.9 %reduce-scatter.2.cloned.1.call-start = ((), (), s32[]{:S(2)}) async-start(), calls=%async_computation.3 | async-start | bytes 5242880 | tf_op jit(solution)/shard_map/reduce_scatter | solution.py:175
  9.7 6.1 %copy-start.17 = (f32[2]{0:T(128)}, f32[2]{0:T(128)S(1)}, u32[]{:S(2)}) copy-start(f32[2]{0:T(128)S(1)} %get-tuple-element.2591) | copy-start | bytes 28
  9.7 6.1 %copy-start.19 = (f32[2]{0:T(128)}, f32[2]{0:T(128)S(1)}, u32[]{:S(2)}) copy-start(f32[2]{0:T(128)S(1)} %get-tuple-element.2592) | copy-start | bytes 28
  10.4 5.4 %copy-start.13 = (f32[1,1,2,256]{3,2,1,0:T(2,128)}, f32[1,1,2,256]{3,2,1,0:T(2,128)S(1)}, u32[]{:S(2)}) copy-start(f32[1,1,2,256]{3,2,1,0:T(2,128)S(1)} %get-tuple-element.2587) | copy-start | bytes 6148
  10.6 5.2 %copy-start.5 = (f32[2,4,64]{2,1,0:T(4,128)}, f32[2,4,64]{2,1,0:T(4,128)S(1)}, u32[]{:S(2)}) copy-start(f32[2,4,64]{2,1,0:T(4,128)S(1)} %squeeze.380) | copy-start | bytes 6148
  11.6 4.2 copy-start.9
  11.7 4.2 copy-start.7
  12.9 2.9 copy-start.11
  77.5 59.6 %copy-start = (f32[1,1,2,128,128]{4,3,2,1,0:T(8,128)S(1)}, f32[1,1,2,128,128]{4,3,2,1,0:T(8,128)}, u32[]{:S(2)}) copy-start(f32[1,1,2,128,128]{4,3,2,1,0:T(8,128)} %param.27) | copy-start | bytes 393220
  228.1 33.5 %copy-start.3 = (pred[64,64]{1,0:T(8,128)(4,1)S(1)}, pred[64,64]{1,0:T(8,128)(4,1)}, u32[]{:S(2)}) copy-start(pred[64,64]{1,0:T(8,128)(4,1)} %iota_compare_fusion.11) | copy-start | bytes 12292
  384.0 0.7 copy-start.6
  384.0 0.7 copy-start.15
  384.0 0.7 copy-start.18
  384.0 0.7 copy-start.20
  384.1 0.9 copy-start.21
  384.1 13.0 %copy-start.2 = (f32[4,2,64,128]{3,2,0,1:T(8,128)S(1)}, f32[4,2,64,128]{3,2,0,1:T(8,128)}, u32[]{:S(2)}) copy-start(f32[4,2,64,128]{3,2,0,1:T(8,128)} %get-tuple-element.1712) | copy-start | bytes 786436
  384.1 13.2 %copy-start.10 = (f32[2,256]{1,0:T(2,128)S(1)}, f32[2,256]{1,0:T(2,128)}, u32[]{:S(2)}) copy-start(f32[2,256]{1,0:T(2,128)} %copy-done.9) | copy-start | bytes 6148
  384.1 13.2 %copy-start.8 = (f32[2,256]{1,0:T(2,128)S(1)}, f32[2,256]{1,0:T(2,128)}, u32[]{:S(2)}) copy-start(f32[2,256]{1,0:T(2,128)} %copy-done.7) | copy-start | bytes 6148
  384.1 14.0 %copy-start.1 = (f32[4,2,64,128]{3,2,0,1:T(8,128)S(1)}, f32[4,2,64,128]{3,2,0,1:T(8,128)}, u32[]{:S(2)}) copy-start(f32[4,2,64,128]{3,2,0,1:T(8,128)} %get-tuple-element.1711) | copy-start | bytes 786436
  384.1 14.2 %copy-start.12 = (f32[2,256]{1,0:T(2,128)S(1)}, f32[2,256]{1,0:T(2,128)}, u32[]{:S(2)}) copy-start(f32[2,256]{1,0:T(2,128)} %copy-done.11) | copy-start | bytes 6148
  384.1 15.1 %copy-start.14 = (f32[1,1,2,256]{3,2,1,0:T(2,128)S(1)}, f32[1,1,2,256]{3,2,1,0:T(2,128)}, u32[]{:S(2)}) copy-start(f32[1,1,2,256]{3,2,1,0:T(2,128)} %copy-done.13) | copy-start | bytes 6148
  384.1 15.1 %copy-start.16 = (f32[2,1,2,256]{3,2,1,0:T(2,128)S(1)}, f32[2,1,2,256]{3,2,1,0:T(2,128)}, u32[]{:S(2)}) copy-start(f32[2,1,2,256]{3,2,1,0:T(2,128)} %param.25) | copy-start | bytes 12292
Sparse Core Ops, SparseCore 0:
  9.6 79.3 all-gather.4
  90.8 38.1 all-gather.6
  384.3 76.1 reduce-scatter.1
where the time goes:
time: 472 us; the launch traced here: 467 us
  other arithmetic  170 us (36%)
  waiting for transfers between devices  114 us (24%)
  matrix products  96.6 us (20%)
  local copies, waits for them, and re-layouts  45.8 us (10%)
  blocking collectives  25.2 us (5%)
  between operations  14.4 us (3%)
    another operation x52, other arithmetic, inner_step(): jax.scipy.linalg.solve_triangular(system, right_side, lower=True, unit_di...  125 us
    reduce_scatter x1, waiting for transfers between devices, per_device(): lax.psum_scatter(lax.dot_general(value_grad, weight_full, (((1,), (1,)),...  60.6 us
    all_gather x1, waiting for transfers between devices, per_device(): lax.all_gather(value_weight, ('dp', 'ctx'), axis=0, tiled=True)  40.1 us
    dynamic_update_slice x24, other arithmetic, core(): lax.scan(inner_step, initial, (into_blocks(query_unit), into_blocks(key_u...  18.9 us
    dot_general x20, matrix products, inner_step(): jnp.dot((key_unit * tail_decay[:, None]).T, new_values, precision=highest)  14.5 us
    all_gather x2, blocking collectives, entering(): lax.all_gather(part.astype(kind), axis)  13.2 us
    dot_general x20, matrix products, inner_step(): jnp.dot(solved[:, :head_dim], carried, precision=highest)  13.2 us
    psum x1, blocking collectives, per_device(): decay_grad = lax.psum(gradients[5], ('dp', 'ctx'))  11.9 us
  transfers between devices with their start and end apart: 3, of which 3 were waited for; matrix products, arithmetic and copies ran while one was open for 14% of the time, Pallas kernels for 0%

commit v1 on v0

v1 whole, which is shorter than its diff:
```python
import functools

import jax
import jax.numpy as jnp
from jax import lax
from jax.experimental import pallas as pl
from jax.experimental.pallas import tpu as pltpu
from jax.sharding import PartitionSpec as P

epsilon = 1e-06
f32, bf16 = jnp.float32, jnp.bfloat16
NN, NT, TN = ((1,), (0,)), ((1,), (1,)), ((0,), (0,))
ROWS = ("dp", "ctx")


def mm(a, b, dims=NN):
    return lax.dot_general(
        a.astype(bf16), b.astype(bf16), (dims, ((), ())), preferred_element_type=f32
    )


def halves(a):
    high = a.astype(bf16)
    return high, (a - high.astype(f32)).astype(bf16)


def mm3(a, b):
    (ah, al), (bh, bl) = a, b
    return mm(ah, bh) + (mm(ah, bl) + mm(al, bh))


def grid_of(n):
    rows = lax.broadcasted_iota(jnp.int32, (n, n), 0)
    cols = lax.broadcasted_iota(jnp.int32, (n, n), 1)
    return rows, cols


def to_col(row, eye):
    return jnp.sum(jnp.where(eye, row, 0.0), axis=1, keepdims=True)


def to_row(col, eye):
    return jnp.sum(jnp.where(eye, col, 0.0), axis=0, keepdims=True)


def decay_of(log_row, rows, cols):
    cum = jnp.sum(jnp.where(cols <= rows, log_row, 0.0), axis=1, keepdims=True)
    cum_row = to_row(cum, rows == cols)
    lower = rows >= cols
    decays = jnp.where(lower, jnp.exp(jnp.where(lower, cum - cum_row, 0.0)), 0.0)
    last = cum[-1:, :]
    return decays, jnp.exp(cum), jnp.exp(last - cum), jnp.exp(last)


def unit(raw):
    raw = raw.astype(f32)
    inv = lax.rsqrt(jnp.sum(raw * raw, axis=1, keepdims=True) + epsilon)
    return raw * inv, inv


def inverse(system, rows, cols):
    size, n = 1, system.shape[0]
    result = jnp.where(rows == cols, 1.0, 0.0)
    while size < n:
        pair = jnp.logical_and(rows // (2 * size) == cols // (2 * size), rows // size > cols // size)
        part = jnp.where(pair, system, 0.0)
        if size == 1:
            result = result - part
        else:
            split = halves(result)
            result = result - mm3(split, halves(mm3(halves(part), split)))
        size *= 2
    return result


def maps_kernel(heads, q_ref, k_ref, do_ref, gate_ref, maps_ref, solve_ref):
    n, width = q_ref.shape
    d = width // heads
    rows, cols = grid_of(n)
    srows, scols = grid_of(d)
    for h in range(heads):
        at = slice(h * d, (h + 1) * d)
        query = unit(q_ref[:, at])[0] * d**-0.5
        key = unit(k_ref[:, at])[0]
        do = do_ref[:, at]
        decays, grow, tail, total = decay_of(gate_ref[h : h + 1, :], rows, cols)
        strength = to_col(gate_ref[heads + h : heads + h + 1, :], rows == cols)
        system = jnp.where(rows > cols, strength * decays * mm(key, key, NT), 0.0)
        solve = inverse(system, rows, cols)
        solve_ref[h] = solve.astype(bf16)
        scores = decays * mm(query, key, NT)
        weights = mm(solve, strength * grow * key)
        matrix = jnp.where(srows == scols, total, 0.0) - mm(weights, tail * key, TN)
        local = mm(grow * query, do, TN) - mm(weights, mm(scores, do, TN), TN)
        maps_ref[h, 0] = matrix.astype(bf16)
        maps_ref[h, 1] = local.astype(bf16)


def value_kernel(
    heads, place_ref, q_ref, k_ref, do_ref, gate_ref, solve_ref, all_ref, dv_ref, dr_ref, inc_ref
):
    n, width = q_ref.shape
    d = width // heads
    place = place_ref[0]
    rows, cols = grid_of(n)
    for h in range(heads):
        at = slice(h * d, (h + 1) * d)
        incoming = jnp.zeros((d, d), f32)
        for later in reversed(range(1, all_ref.shape[0])):
            high, low = halves(incoming)
            matrix = all_ref[later, h, 0]
            new = mm(matrix, high) + mm(matrix, low) + all_ref[later, h, 1].astype(f32)
            incoming = jnp.where(later > place, new, incoming)
        inc_ref[h] = incoming
        query = unit(q_ref[:, at])[0] * d**-0.5
        key = unit(k_ref[:, at])[0]
        decays, grow, tail, total = decay_of(gate_ref[h : h + 1, :], rows, cols)
        strength = to_col(gate_ref[heads + h : heads + h + 1, :], rows == cols)
        scores = decays * mm(query, key, NT)
        dn = mm(scores, do_ref[:, at], TN) + mm(tail * key, incoming)
        dr = mm(solve_ref[h], dn, TN)
        dr_ref[:, at] = dr
        dv_ref[:, at] = (strength * dr).astype(bf16)


def grads_kernel(
    heads, q_ref, k_ref, do_ref, gate_ref, solve_ref, dr_ref, inc_ref, state_ref, v_ref,
    dq_ref, dk_ref, dgate_ref,
):
    n, width = q_ref.shape
    d = width // heads
    rows, cols = grid_of(n)
    eye = rows == cols
    lower = rows >= cols
    strict = rows > cols
    scale = d**-0.5

    def gate(kind, h):
        return gate_ref[kind * heads + h : kind * heads + h + 1, :]

    def rowsum(a):
        return jnp.sum(a, axis=1, keepdims=True)

    for h in range(heads):
        at = slice(h * d, (h + 1) * d)
        qh, qinv = unit(q_ref[:, at])
        key, kinv = unit(k_ref[:, at])
        query = qh * scale
        do = do_ref[:, at]
        decays, grow, tail, total = decay_of(gate(0, h), rows, cols)
        strength = to_col(gate(1, h), eye)
        state = state_ref[h]
        incoming = inc_ref[h]
        dr = dr_ref[:, at]
        held = mm(key, state)
        gap = v_ref[:, at].astype(f32) - grow * held
        new = mm(solve_ref[h], strength * gap)
        from_state = mm(do, state, NT)
        dscores = jnp.where(lower, mm(do, new, NT), 0.0)
        dsystem = jnp.where(strict, -mm(dr, new, NT), 0.0)
        gram = mm(key, key, NT)
        scores = decays * mm(query, key, NT)
        ds = dscores * decays
        dsd = dsystem * decays
        dgram = dsd * strength
        dq = grow * from_state + mm(ds, key)
        new_inc = mm(new, incoming, NT)
        dk = (
            tail * new_inc
            + mm(ds, query, TN)
            - strength * grow * mm(dr, state, NT)
            + mm(dgram, key)
            + mm(dgram, key, TN)
        )
        mix = dsd * gram
        dstrength = rowsum(dr * gap) + rowsum(mix)
        spread = dscores * scores + mix * strength
        tails = tail * rowsum(key * new_inc)
        dcum = (
            grow * (rowsum(query * from_state) - strength * rowsum(dr * held))
            + rowsum(spread)
            - tails
            - to_col(jnp.sum(spread, axis=0, keepdims=True), eye)
        )
        end = jnp.sum(tails, axis=0, keepdims=True) + total * jnp.sum(
            rowsum(incoming * state), axis=0, keepdims=True
        )
        dlog = jnp.sum(jnp.where(lower, dcum, 0.0), axis=0, keepdims=True) + end
        dq_ref[:, at] = (qinv * scale * (dq - qh * rowsum(qh * dq))).astype(bf16)
        dk_ref[:, at] = (kinv * (dk - key * rowsum(key * dk))).astype(bf16)
        dgate_ref[h : h + 1, :] = dlog * gate(2, h)
        dgate_ref[heads + h : heads + h + 1, :] = to_row(dstrength, eye) * gate(3, h)
        dgate_ref[2 * heads + h : 2 * heads + h + 1, :] = dlog * gate(0, h)


def call(kernel, outs, in_count, flops, smem=0):
    return pl.pallas_call(
        kernel,
        out_shape=outs,
        in_specs=[pl.BlockSpec(memory_space=pltpu.SMEM)] * smem
        + [pl.BlockSpec(memory_space=pltpu.VMEM)] * in_count,
        out_specs=[pl.BlockSpec(memory_space=pltpu.VMEM)] * len(outs),
        compiler_params=pltpu.CompilerParams(vmem_limit_bytes=32 * 1024 * 1024),
        cost_estimate=pl.CostEstimate(flops=flops, bytes_accessed=2**21, transcendentals=2**17),
    )


def per_device(
    layer_input, value_weight, query_raw, key_raw, out_grad, gate_logits, decay_params, saved_states
):
    tp = lax.axis_size("tp")
    shape = jax.ShapeDtypeStruct
    query, key, do = query_raw[0], key_raw[0], out_grad[0]
    n, width = query.shape
    d = saved_states.shape[-1]
    heads = width // d
    tokens = layer_input.shape[1]

    weights = lax.all_gather(value_weight, "tp")
    sliced = lax.all_to_all(layer_input[0], ROWS, split_axis=1, concat_axis=0, tiled=True)

    scale = -jnp.exp(decay_params[0])[:, None]
    logit = gate_logits[0, 0] + decay_params[1][:, None]
    strength = jax.nn.sigmoid(gate_logits[1, 0])
    gates = jnp.concatenate(
        [
            scale * jax.nn.softplus(logit),
            strength,
            scale * jax.nn.sigmoid(logit),
            strength * (1.0 - strength),
        ]
    )
    maps, solve = call(
        functools.partial(maps_kernel, heads),
        [shape((heads, 2, d, d), bf16), shape((heads, n, n), bf16)],
        4,
        2**33,
    )(query, key, do, gates)
    everything = lax.all_gather(maps, "ctx")
    place = lax.axis_index("ctx").astype(jnp.int32)[None]
    dv, dr, incoming = call(
        functools.partial(value_kernel, heads),
        [shape((n, width), bf16), shape((n, width), f32), shape((heads, d, d), f32)],
        6,
        2**31,
        1,
    )(place, query, key, do, gates, solve, everything)

    partial = lax.dot_general(
        sliced, weights, (((1,), (1,)), ((), ())), preferred_element_type=f32
    ).astype(bf16)
    summed = lax.psum_scatter(partial, ROWS, scatter_dimension=0, tiled=True)
    values = lax.all_to_all(summed, "tp", split_axis=1, concat_axis=0, tiled=True)
    values = values.reshape(n, width)

    turned = lax.all_to_all(dv.reshape(tp, tokens, width), "tp", split_axis=0, concat_axis=0)
    wide = lax.all_gather(turned.reshape(tp, tokens, width), ROWS)
    product = jnp.einsum("ntlc,tdc->nld", wide, weights, preferred_element_type=f32).astype(bf16)
    input_grad = lax.all_to_all(product, ROWS, split_axis=0, concat_axis=2, tiled=True)
    input_grad = input_grad.reshape(1, tokens, layer_input.shape[2])

    dq, dk, dgate = call(
        functools.partial(grads_kernel, heads),
        [shape((n, width), bf16), shape((n, width), bf16), shape((3 * heads, n), f32)],
        9,
        2**32,
    )(query, key, do, gates, solve, dr, incoming, saved_states[0, 0], values)
    gate_grad = dgate[: 2 * heads].reshape(2, 1, heads, n)
    sums = jnp.sum(dgate.reshape(3, heads, n), axis=2)
    decay_grad = lax.psum(jnp.stack([sums[2], sums[0]]), ROWS)
    return (input_grad, dq[None], dk[None], gate_grad, decay_grad)


def solution(mesh):
    placed = (
        P("dp", ("ctx", "tp"), None),
        P(("dp", "ctx"), "tp"),
        P("dp", "ctx", "tp"),
        P("dp", "ctx", "tp"),
        P("dp", "ctx", "tp"),
        P(None, "dp", "tp", "ctx"),
        P(None, "tp"),
        P("dp", "ctx", "tp", None, None),
    )
    return jax.shard_map(
        per_device,
        mesh=mesh,
        in_specs=placed,
        out_specs=(
            P("dp", ("ctx", "tp"), None),
            P("dp", "ctx", "tp"),
            P("dp", "ctx", "tp"),
            P(None, "dp", "tp", "ctx"),
            P(None, "tp"),
        ),
        check_vma=False,
    )
```

time: 472 us -> 158 us (0.33)
  other arithmetic: 170 us -> 1.69 us
  matrix products: 96.6 us -> 7.02 us
  waiting for transfers between devices: 114 us -> 39.3 us
  blocking collectives: 25.2 us -> 69 us
  local copies, waits for them, and re-layouts: 45.8 us -> 5.66 us
  Pallas kernels: 0 us -> 14.3 us
    another operation x86 -> x1, other arithmetic: 132 us -> 0.01 us  [per_device(): decay_grad = lax.psum(jnp.stack([sums[2], sums[0]]), ROWS)]
    dot_general x102 -> x2, matrix products: 85.4 us -> 7.02 us  [the longest x1 3.82 us: per_device(): lax.dot_general(sliced, weights, (((1,), (1,)), ((), ())), preferred_elem...]
    all_to_all x0 -> x3, blocking collectives: none -> 47.1 us  [the longest x1 18.1 us: per_device(): lax.all_to_all(layer_input[0], ROWS, split_axis=1, concat_axis=0, tiled=T...]
    reduce_scatter x1, waiting for transfers between devices: 60.6 us -> 19 us  [per_device(): summed = lax.psum_scatter(partial, ROWS, scatter_dimension=0, tiled=True)]
    all_gather x2, waiting for transfers between devices: 51.5 us -> 16.3 us  [the longest x1 16.3 us: per_device(): wide = lax.all_gather(turned.reshape(tp, tokens, width), ROWS)]
    dynamic_update_slice x24 -> x0, other arithmetic: 18.9 us -> none  [core(): lax.scan(inner_step, initial, (into_blocks(query_unit), into_blocks(key_u...]
    pallas_call x0 -> x3, Pallas kernels: none -> 14.3 us  [the longest x1 10.2 us: per_device(): call(functools.partial(maps_kernel, heads), [shape((heads, 2, d, d), bf16...]
    mul x26 -> x0, local copies, waits for them, and re-layouts: 13.2 us -> none  [the longest x8 4.82 us: inner_step(): jnp.exp(cumulative[-1]) * carried]
  transfers between devices with their start and end apart: 3 -> 4, of which waited for: 3 -> 3; matrix products, arithmetic and copies ran while one was open for 14% -> 7% of each run, Pallas kernels for 0% -> 8%
where the time goes in v1:
time: 158 us; the launch traced here: 155 us
  blocking collectives  69 us (44%)
  waiting for transfers between devices  39.3 us (25%)
  Pallas kernels  14.3 us (9%)
  between operations  13.9 us (9%)
  matrix products  7.02 us (4%)
  local copies, waits for them, and re-layouts  5.66 us (4%)
  starting transfers between devices  4.69 us (3%)
  other arithmetic  1.69 us (1%)
    reduce_scatter x1, waiting for transfers between devices, per_device(): summed = lax.psum_scatter(partial, ROWS, scatter_dimension=0, tiled=True)  19 us
    all_to_all x1, blocking collectives, per_device(): lax.all_to_all(layer_input[0], ROWS, split_axis=1, concat_axis=0, tiled=T...  18.1 us
    all_to_all x1, blocking collectives, per_device(): lax.all_to_all(product, ROWS, split_axis=0, concat_axis=2, tiled=True)  16.8 us
    all_gather x1, waiting for transfers between devices, per_device(): wide = lax.all_gather(turned.reshape(tp, tokens, width), ROWS)  16.3 us
    psum x1, blocking collectives, per_device(): decay_grad = lax.psum(jnp.stack([sums[2], sums[0]]), ROWS)  14.2 us
    all_to_all x1, blocking collectives, per_device(): lax.all_to_all(dv.reshape(tp, tokens, width), 'tp', split_axis=0, concat_...  12.3 us
    pallas_call x1, Pallas kernels, per_device(): call(functools.partial(maps_kernel, heads), [shape((heads, 2, d, d), bf16...  10.2 us
    all_gather x1, blocking collectives, per_device(): everything = lax.all_gather(maps, 'ctx')  7.71 us
  transfers between devices with their start and end apart: 4, of which 3 were waited for; matrix products, arithmetic and copies ran while one was open for 7% of the time, Pallas kernels for 8%

profile of v1, /device:TPU:9, one launch (start us, length us, event | category | flops | bytes accessed | tf_op | source)
XLA Modules:
  0.0 155.5 jit_solution(15280650308774004236)
XLA Ops:
  7.2 0.0 all-gather.8.cloned.1.call-start
  7.2 0.7 all-gather.8.cloned.1.call-update
  7.9 0.0 all-gather.6.cloned.1.call-start
  8.0 0.8 negate_bitcast_fusion
  8.7 0.8 fusion
  9.5 0.0 copy-start
  9.5 0.9 copy-done
  10.4 0.9 copy-done.2
  11.3 0.9 copy-done.4
  12.2 10.2 %shard_map.119 = (bf16[2,2,128,128]{3,2,1,0:T(8,128)(2,1)S(1)}, bf16[2,256,256]{2,1,0:T(8,128)(2,1)S(1)}) custom-call(bf16[256,256]{1,0:T(8,128)(2,1)S(1)} %bitcast.59, bf16[256,256]{1,0:T(8,128)(2,1)S(1)} %bitcast.62, bf16[256,256]{1,0:T(8,128)(2,1)S(1)} %bitcast.65, f32[8,256]{1,0:T(8,128)S(1)} %pad_maximum_fusion.gate_ref), custom_call_target="tpu_custom_call" | custom-call | flops 8589934592 | bytes 2097152 | tf_op jit(solution)/shard_map/pallas_call | solution.py:233
  22.4 7.7 %all-gather = bf16[8,2,128,128]{3,2,1,0:T(8,128)(2,1)S(1)} all-gather(bf16[2,2,128,128]{3,2,1,0:T(8,128)(2,1)S(1)} %get-tuple-element.14), channel_id=2, replica_groups=mesh['dp'=2,'ctx'=4,'tp'=4] {'ctx'}, dimensions={0}, use_global_device_ids=true | all-gather | bytes 655360 | tf_op jit(solution)/shard_map/all_gather | solution.py:239
  30.2 1.6 %shard_map.120 = (bf16[256,256]{1,0:T(8,128)(2,1)S(1)}, f32[256,256]{1,0:T(8,128)S(1)}, f32[2,128,128]{2,1,0:T(8,128)S(1)}) custom-call(s32[1]{0:T(128)} %bitcast.place_ref, bf16[256,256]{1,0:T(8,128)(2,1)S(1)} %bitcast.60, bf16[256,256]{1,0:T(8,128)(2,1)S(1)} %bitcast.63, bf16[256,256]{1,0:T(8,128)(2,1)S(1)} %bitcast.66, ...), custom_call_target="tpu_custom_call" | custom-call | flops 2147483648 | bytes 2097152 | tf_op jit(solution)/shard_map/pallas_call | solution.py:241
  31.8 12.3 %all_to_all.57 = bf16[4,64,256]{2,1,0:T(8,128)(2,1)} all-to-all(bf16[4,64,256]{2,1,0:T(8,128)(2,1)S(1)} %bitcast.58), channel_id=1, replica_groups=mesh['dp'=2,'ctx'=4,'tp'=4] {'tp'}, dimensions={0} | all-to-all | bytes 262144 | tf_op jit(solution)/shard_map/all_to_all | solution.py:256
  44.1 0.0 all-gather.6.cloned.1.call-update
  44.1 0.0 reduce-scatter.2.cloned.1.call-start
  44.2 0.6 copy.23
  44.8 0.6 copy.19
  45.4 18.1 %all_to_all.58 = bf16[64,8,1024]{2,0,1:T(8,128)(2,1)S(1)} all-to-all(bf16[64,8,1024]{2,0,1:T(8,128)(2,1)S(1)} %copy.19), channel_id=1, replica_groups=mesh['dp'=2,'ctx'=4,'tp'=4] {'dp','ctx'}, dimensions={1} | all-to-all | bytes 2097152 | tf_op jit(solution)/shard_map/all_to_all | solution.py:220
  63.4 3.8 %convolution_convert_fusion = bf16[512,4,256]{2,0,1:T(8,128)(2,1)} fusion(bf16[512,1024,1]{1,0,2:T(8,128)(2,1)S(1)} %bitcast.73, bf16[4,1024,256]{2,1,0:T(8,128)(2,1)} %bitcast.75), kind=kOutput, calls=%fused_computation.1 | convolution fusion | flops 1074266112 | bytes 4194304 | tf_op jit(solution)/shard_map/dot_general | solution.py:249
  67.2 0.0 reduce-scatter.2.cloned.1.call-update
  67.3 16.3 %all-gather.6.cloned.1.call-done = bf16[32,64,256]{2,1,0:T(8,128)(2,1)} async-done(((bf16[4,64,256]{2,1,0:T(8,128)(2,1)}), bf16[32,64,256]{2,1,0:T(8,128)(2,1)}) %all-gather.6.cloned.1.call-update) | async-done | bytes 1048592 | tf_op jit(solution)/shard_map/all_gather | solution.py:257
  83.6 3.2 %bitcast_convert_fusion = bf16[8,64,1024]{2,1,0:T(8,128)(2,1)S(1)} fusion(bf16[8,4,64,256]{3,2,1,0:T(8,128)(2,1)} %bitcast.77, bf16[4,1024,256,1]{2,1,0,3:T(8,128)(2,1)} %bitcast.76), kind=kOutput, calls=%fused_computation | convolution fusion | flops 1074266112 | bytes 4194304 | tf_op jit(solution)/shard_map/ntlc,tdc->nld/dot_general | solution.py:258
  86.8 16.8 %all_to_all.59 = bf16[8,64,1024]{2,1,0:T(8,128)(2,1)S(1)} all-to-all(bf16[8,64,1024]{2,1,0:T(8,128)(2,1)S(1)} %bitcast_convert_fusion), channel_id=1, replica_groups=mesh['dp'=2,'ctx'=4,'tp'=4] {'dp','ctx'}, dimensions={0} | all-to-all | bytes 2097152 | tf_op jit(solution)/shard_map/all_to_all | solution.py:259
  103.6 19.0 %reduce-scatter.2.cloned.1.call-done = bf16[64,4,256]{2,0,1:T(8,128)(2,1)} async-done(((bf16[512,4,256]{2,0,1:T(8,128)(2,1)}), bf16[64,4,256]{2,0,1:T(8,128)(2,1)}) %reduce-scatter.2.cloned.1.call-update) | async-done | bytes 131088 | tf_op jit(solution)/shard_map/reduce_scatter | solution.py:252
  122.6 4.6 %all-to-all-start.3 = ((bf16[64,4,256]{2,0,1:T(8,128)(2,1)}), bf16[64,4,256]{2,0,1:T(8,128)(2,1)S(1)}, u32[]{:S(2)}, u32[]{:S(2)}) async-start(bf16[64,4,256]{2,0,1:T(8,128)(2,1)} %reduce-scatter.2.cloned.1.call-done), calls=%async_computation.4 | async-start | bytes 262144 | tf_op jit(solution)/shard_map/all_to_all | solution.py:253
  127.1 1.1 copy.22
  128.2 3.2 %all-to-all-done.3 = bf16[64,4,256]{2,0,1:T(8,128)(2,1)S(1)} async-done(((bf16[64,4,256]{2,0,1:T(8,128)(2,1)}), bf16[64,4,256]{2,0,1:T(8,128)(2,1)S(1)}, u32[]{:S(2)}, u32[]{:S(2)}) %all-to-all-start.3) | async-done | bytes 131104 | tf_op jit(solution)/shard_map/all_to_all | solution.py:253
  131.5 2.5 %shard_map.121 = (bf16[256,256]{1,0:T(8,128)(2,1)}, bf16[256,256]{1,0:T(8,128)(2,1)}, f32[6,256]{1,0:T(8,128)S(1)}) custom-call(bf16[256,256]{1,0:T(8,128)(2,1)S(1)} %bitcast.61, bf16[256,256]{1,0:T(8,128)(2,1)S(1)} %bitcast.64, bf16[256,256]{1,0:T(8,128)(2,1)S(1)} %bitcast.67, f32[8,256]{1,0:T(8,128)S(1)} %pad_maximum_fusion.gate_ref, ...), custom_call_target="tpu_custom_call" | custom-call | flops 4294967296 | bytes 2097152 | tf_op jit(solution)/shard_map/pallas_call | solution.py:262
  134.0 0.1 reduce_sum.9
  134.1 0.1 slice_bitcast_fusion.1
  134.2 14.2 %psum.7 = f32[2,2]{1,0:T(2,128)} all-reduce(f32[2,2]{1,0:T(2,128)S(1)} %pad_maximum_fusion.1), channel_id=1, replica_groups=mesh['dp'=2,'ctx'=4,'tp'=4] {'dp','ctx'}, use_global_device_ids=true, to_apply=%region_2.3 | all-reduce | flops 4 | bytes 32 | tf_op jit(solution)/shard_map/psum | solution.py:270
  148.4 0.6 reshape.46
  (16 shorter events, 0.1 us)
Async XLA Ops:
  7.2 56.3 %all-gather.8.cloned.1.call-start = ((), (), s32[]{:S(2)}) async-start(), calls=%async_computation.7 | async-start | bytes 2621440 | tf_op jit(solution)/shard_map/all_gather | solution.py:219
  7.9 75.7 %all-gather.6.cloned.1.call-start = ((), (), s32[]{:S(2)}) async-start(), calls=%async_computation.6 | async-start | bytes 1179648 | tf_op jit(solution)/shard_map/all_gather | solution.py:257
  9.5 0.9 copy-start
  10.4 0.9 copy-start.2
  11.3 0.9 copy-start.4
  30.2 14.0 %copy-start.7 = (bf16[1,64,8192]{2,1,0:T(8,128)(2,1)S(1)}, bf16[1,64,8192]{2,1,0:T(8,128)(2,1)}, u32[]{:S(2)}) copy-start(bf16[1,64,8192]{2,1,0:T(8,128)(2,1)} %param.8) | copy-start | bytes 3145732
  44.1 78.5 %reduce-scatter.2.cloned.1.call-start = ((), (), s32[]{:S(2)}) async-start(), calls=%async_computation.5 | async-start | bytes 1179648 | tf_op jit(solution)/shard_map/reduce_scatter | solution.py:252
  86.8 44.7 %copy-start.1 = (bf16[1,256,256]{2,1,0:T(8,128)(2,1)S(1)}, bf16[1,256,256]{2,1,0:T(8,128)(2,1)}, u32[]{:S(2)}) copy-start(bf16[1,256,256]{2,1,0:T(8,128)(2,1)} %param.10) | copy-start | bytes 393220
  86.8 44.7 %copy-start.3 = (bf16[1,256,256]{2,1,0:T(8,128)(2,1)S(1)}, bf16[1,256,256]{2,1,0:T(8,128)(2,1)}, u32[]{:S(2)}) copy-start(bf16[1,256,256]{2,1,0:T(8,128)(2,1)} %param.11) | copy-start | bytes 393220
  86.8 44.7 %copy-start.5 = (bf16[1,256,256]{2,1,0:T(8,128)(2,1)S(1)}, bf16[1,256,256]{2,1,0:T(8,128)(2,1)}, u32[]{:S(2)}) copy-start(bf16[1,256,256]{2,1,0:T(8,128)(2,1)} %param.12) | copy-start | bytes 393220
  86.8 44.7 %copy-start.6 = (f32[1,1,2,128,128]{4,3,2,1,0:T(8,128)S(1)}, f32[1,1,2,128,128]{4,3,2,1,0:T(8,128)}, u32[]{:S(2)}) copy-start(f32[1,1,2,128,128]{4,3,2,1,0:T(8,128)} %param.15) | copy-start | bytes 393220
  122.6 8.9 %all-to-all-start.3 = ((bf16[64,4,256]{2,0,1:T(8,128)(2,1)}), bf16[64,4,256]{2,0,1:T(8,128)(2,1)S(1)}, u32[]{:S(2)}, u32[]{:S(2)}) async-start(bf16[64,4,256]{2,0,1:T(8,128)(2,1)} %reduce-scatter.2.cloned.1.call-done), calls=%async_computation.4 | async-start | bytes 262144 | tf_op jit(solution)/shard_map/all_to_all | solution.py:253
Sparse Core Ops, SparseCore 0:
  9.5 47.2 all-gather.7
  58.7 24.8 all-gather.5
  87.3 35.1 reduce-scatter.1

commit v2 on v1

--- a/solution.py
+++ b/solution.py
@@ -205,6 +205,87 @@
     )
 
 
+def spot_of(axes, flat):
+    spot = {}
+    for name in reversed(axes):
+        size = lax.axis_size(name)
+        spot[name] = lax.rem(flat, size)
+        flat = flat // size
+    return spot
+
+
+def exchange_kernel(axes, share, count, src_ref, dst_ref, send_sem, recv_sem, own_sem):
+    me = jnp.int32(0)
+    for name in axes:
+        me = me * lax.axis_size(name) + lax.axis_index(name)
+    barrier = pltpu.get_barrier_semaphore()
+
+    def greet(step, carry):
+        peer = lax.rem(me + step, count)
+        pl.semaphore_signal(
+            barrier, inc=1, device_id=spot_of(axes, peer), device_id_type=pl.DeviceIdType.MESH
+        )
+        return carry
+
+    lax.fori_loop(1, count, greet, 0)
+    own = pltpu.make_async_copy(src_ref.at[me // share], dst_ref.at[me], own_sem)
+    own.start()
+    pl.semaphore_wait(barrier, count - 1)
+
+    def copy_of(step):
+        peer = lax.rem(me + step, count)
+        return pltpu.make_async_remote_copy(
+            src_ref=src_ref.at[peer // share],
+            dst_ref=dst_ref.at[me],
+            send_sem=send_sem.at[step],
+            recv_sem=recv_sem.at[step],
+            device_id=spot_of(axes, peer),
+            device_id_type=pl.DeviceIdType.MESH,
+        )
+
+    def begin(step, carry):
+        copy_of(step).start()
+        return carry
+
+    def finish(step, carry):
+        source = lax.rem(me + count - step, count)
+        pltpu.make_async_remote_copy(
+            src_ref=src_ref.at[lax.rem(me + step, count) // share],
+            dst_ref=dst_ref.at[source],
+            send_sem=send_sem.at[step],
+            recv_sem=recv_sem.at[step],
+            device_id=spot_of(axes, lax.rem(me + step, count)),
+            device_id_type=pl.DeviceIdType.MESH,
+        ).wait()
+        return carry
+
+    lax.fori_loop(1, count, begin, 0)
+    own.wait()
+    lax.fori_loop(1, count, finish, 0)
+
+
+def exchange(source, axes, number, share=1):
+    count = 1
+    for name in axes:
+        count *= lax.axis_size(name)
+    block = source.shape[1:]
+    return pl.pallas_call(
+        functools.partial(exchange_kernel, axes, share, count),
+        out_shape=jax.ShapeDtypeStruct((count, *block), source.dtype),
+        in_specs=[pl.BlockSpec(memory_space=pltpu.VMEM)],
+        out_specs=pl.BlockSpec(memory_space=pltpu.VMEM),
+        scratch_shapes=[
+            pltpu.SemaphoreType.DMA((count,)),
+            pltpu.SemaphoreType.DMA((count,)),
+            pltpu.SemaphoreType.DMA,
+        ],
+        compiler_params=pltpu.CompilerParams(
+            collective_id=number, has_side_effects=True, vmem_limit_bytes=32 * 1024 * 1024
+        ),
+        cost_estimate=pl.CostEstimate(flops=2**33, bytes_accessed=2**22, transcendentals=0),
+    )(source)
+
+
 def per_device(
     layer_input, value_weight, query_raw, key_raw, out_grad, gate_logits, decay_params, saved_states
 ):
@@ -246,18 +327,17 @@
         1,
     )(place, query, key, do, gates, solve, everything)
 
-    partial = lax.dot_general(
-        sliced, weights, (((1,), (1,)), ((), ())), preferred_element_type=f32
-    ).astype(bf16)
-    summed = lax.psum_scatter(partial, ROWS, scatter_dimension=0, tiled=True)
-    values = lax.all_to_all(summed, "tp", split_axis=1, concat_axis=0, tiled=True)
+    rows = lax.axis_size("dp") * lax.axis_size("ctx")
+    everyone = ("tp", *ROWS)
+    wide = exchange(dv.reshape(tp, tokens, width), everyone, 0, rows)
+    wide = wide.reshape(tp, rows, tokens, width)
+    product = jnp.einsum("tnlc,tdc->nld", wide, weights, preferred_element_type=f32).astype(bf16)
+    partial = jnp.einsum("nd,tdc->tnc", sliced, weights, preferred_element_type=f32).astype(bf16)
+    parts = exchange(partial.reshape(tp * rows, tokens, width), everyone, 1)
+    values = jnp.sum(parts.reshape(tp, rows, tokens, width).astype(f32), axis=1).astype(bf16)
     values = values.reshape(n, width)
-
-    turned = lax.all_to_all(dv.reshape(tp, tokens, width), "tp", split_axis=0, concat_axis=0)
-    wide = lax.all_gather(turned.reshape(tp, tokens, width), ROWS)
-    product = jnp.einsum("ntlc,tdc->nld", wide, weights, preferred_element_type=f32).astype(bf16)
-    input_grad = lax.all_to_all(product, ROWS, split_axis=0, concat_axis=2, tiled=True)
-    input_grad = input_grad.reshape(1, tokens, layer_input.shape[2])
+    turned = exchange(product, ROWS, 2)
+    input_grad = turned.transpose(1, 0, 2).reshape(1, tokens, layer_input.shape[2])
 
     dq, dk, dgate = call(
         functools.partial(grads_kernel, heads),
@@ -267,7 +347,9 @@
     )(query, key, do, gates, solve, dr, incoming, saved_states[0, 0], values)
     gate_grad = dgate[: 2 * heads].reshape(2, 1, heads, n)
     sums = jnp.sum(dgate.reshape(3, heads, n), axis=2)
-    decay_grad = lax.psum(jnp.stack([sums[2], sums[0]]), ROWS)
+    local = jnp.stack([sums[2], sums[0]])
+    local = jnp.pad(local, ((0, 6), (0, 128 - heads)))[None]
+    decay_grad = jnp.sum(exchange(local, ROWS, 3, rows)[:, :2, :heads], axis=0)
     return (input_grad, dq[None], dk[None], gate_grad, decay_grad)
 
 

time: 158 us -> 149 us (0.943); the launches traced: 155 us -> 149 us
  Pallas kernels: 14.3 us -> 107 us
  blocking collectives: 69 us -> 7.73 us
  waiting for transfers between devices: 39.3 us -> 0.7 us
  local copies, waits for them, and re-layouts: 5.66 us -> 7.46 us
    pallas_call x0 -> x4, Pallas kernels: none -> 92.2 us  [exchange(): pl.pallas_call(functools.partial(exchange_kernel, axes, share, count), ou...]
    all_to_all x3 -> x0, blocking collectives: 47.1 us -> none  [the longest x1 18.1 us: per_device(): lax.all_to_all(layer_input[0], ROWS, split_axis=1, concat_axis=0, tiled=T...]
    reduce_scatter x1 -> x0, waiting for transfers between devices: 19 us -> none  [per_device(): summed = lax.psum_scatter(partial, ROWS, scatter_dimension=0, tiled=True)]
    all_gather x1 -> x0, waiting for transfers between devices: 16.3 us -> none  [per_device(): wide = lax.all_gather(turned.reshape(tp, tokens, width), ROWS)]
    psum x1 -> x0, blocking collectives: 14.2 us -> none  [per_device(): decay_grad = lax.psum(jnp.stack([sums[2], sums[0]]), ROWS)]
    all_to_all x1, waiting for transfers between devices: 3.25 us -> 0.01 us  [per_device(): lax.all_to_all(layer_input[0], ROWS, split_axis=1, concat_axis=0, tiled=T...]
    unnamed x17 -> x13, local copies, waits for them, and re-layouts: 3.34 us -> 1.86 us
  transfers between devices with their start and end apart: 4 -> 2, of which waited for: 3 -> 0; matrix products, arithmetic and copies ran while one was open for 7% -> 2% of each run, Pallas kernels for 8% -> 35%
where the time goes in v2:
time: 149 us
  Pallas kernels  107 us (72%)
  between operations  14.2 us (10%)
  blocking collectives  7.73 us (5%)
  local copies, waits for them, and re-layouts  7.46 us (5%)
  matrix products  6.73 us (5%)
  starting transfers between devices  4.43 us (3%)
    pallas_call x4, Pallas kernels, exchange(): pl.pallas_call(functools.partial(exchange_kernel, axes, share, count), ou...  92.2 us
    pallas_call x1, Pallas kernels, per_device(): call(functools.partial(maps_kernel, heads), [shape((heads, 2, d, d), bf16...  10.2 us
    all_gather x1, blocking collectives, per_device(): everything = lax.all_gather(maps, 'ctx')  7.73 us
    all_to_all x1, starting transfers between devices, per_device(): lax.all_to_all(layer_input[0], ROWS, split_axis=1, concat_axis=0, tiled=T...  4.39 us
    dot_general x1, matrix products, per_device(): jnp.einsum('nd,tdc->tnc', sliced, weights, preferred_element_type=f32)  3.86 us
  transfers between devices with their start and end apart: 2, of which 0 were waited for; matrix products, arithmetic and copies ran while one was open for 2% of the time, Pallas kernels for 35%

profile of v2, /device:TPU:9, one launch (start us, length us, event | category | flops | bytes accessed | tf_op | source)
XLA Modules:
  0.0 148.8 jit_solution(453725525505513690)
XLA Ops:
  7.2 0.0 all-gather.4.cloned.1.call-start
  7.2 0.7 all-gather.4.cloned.1.call-update
  7.9 1.8 %copy.31 = bf16[8,8,8,1024]{3,2,1,0:T(8,128)(2,1)S(1)} copy(bf16[8,8,8,1024]{3,1,2,0:T(8,128)(2,1)} %bitcast.73) | data formatting | bytes 2097152
  9.7 0.0 copy-start.5
  9.7 0.0 copy-start.4
  9.7 0.0 copy-start
  9.8 0.0 copy-start.1
  9.8 0.0 copy-start.2
  9.8 1.5 %copy.25 = bf16[64,8,1024]{2,0,1:T(8,128)(2,1)} copy(bf16[64,8,1024]{2,1,0:T(8,128)(2,1)S(1)} %bitcast.72) | data formatting | bytes 2097152 | tf_op jit(solution)/shard_map/all_to_all | solution.py:301
  11.3 4.4 %all-to-all-start = ((bf16[64,8,1024]{2,0,1:T(8,128)(2,1)}), bf16[64,8,1024]{2,0,1:T(8,128)(2,1)S(1)}, u32[]{:S(2)}, u32[]{:S(2)}) async-start(bf16[64,8,1024]{2,0,1:T(8,128)(2,1)} %copy.25), calls=%async_computation | async-start | bytes 2097152 | tf_op jit(solution)/shard_map/all_to_all | solution.py:301
  15.7 0.1 fusion.2
  15.9 10.2 %shard_map.119 = (bf16[2,2,128,128]{3,2,1,0:T(8,128)(2,1)S(1)}, bf16[2,256,256]{2,1,0:T(8,128)(2,1)S(1)}) custom-call(bf16[256,256]{1,0:T(8,128)(2,1)S(1)} %bitcast.60, bf16[256,256]{1,0:T(8,128)(2,1)S(1)} %bitcast.63, bf16[256,256]{1,0:T(8,128)(2,1)S(1)} %bitcast.66, f32[8,256]{1,0:T(8,128)S(1)} %pad_maximum_fusion.gate_ref), custom_call_target="tpu_custom_call" | custom-call | flops 8589934592 | bytes 2097152 | tf_op jit(solution)/shard_map/pallas_call | solution.py:314
  26.1 7.7 %all-gather = bf16[8,2,128,128]{3,2,1,0:T(8,128)(2,1)S(1)} all-gather(bf16[2,2,128,128]{3,2,1,0:T(8,128)(2,1)S(1)} %get-tuple-element.14), channel_id=2, replica_groups=mesh['dp'=2,'ctx'=4,'tp'=4] {'ctx'}, dimensions={0}, use_global_device_ids=true | all-gather | bytes 655360 | tf_op jit(solution)/shard_map/all_gather | solution.py:320
  33.8 1.6 %shard_map.120 = (bf16[256,256]{1,0:T(8,128)(2,1)S(1)}, f32[256,256]{1,0:T(8,128)S(1)}, f32[2,128,128]{2,1,0:T(8,128)S(1)}) custom-call(s32[1]{0:T(128)} %bitcast.place_ref, bf16[256,256]{1,0:T(8,128)(2,1)S(1)} %bitcast.61, bf16[256,256]{1,0:T(8,128)(2,1)S(1)} %bitcast.64, bf16[256,256]{1,0:T(8,128)(2,1)S(1)} %bitcast.67, ...), custom_call_target="tpu_custom_call" | custom-call | flops 2147483648 | bytes 2097152 | tf_op jit(solution)/shard_map/pallas_call | solution.py:322
  35.4 40.9 %shard_map.121 = bf16[32,64,256]{2,1,0:T(8,128)(2,1)S(1)} custom-call(bf16[4,64,256]{2,1,0:T(8,128)(2,1)S(1)} %bitcast.71), custom_call_target="tpu_custom_call" | custom-call | flops 8589934592 | bytes 4194304 | tf_op jit(solution)/shard_map/pallas_call | solution.py:272
  76.3 0.0 all-to-all-done
  76.3 0.0 all-gather.4.cloned.1.call-done
  76.3 3.9 %fusion = bf16[4,512,256]{1,2,0:T(8,128)(2,1)} fusion(bf16[4,1024,256]{2,1,0:T(8,128)(2,1)} %bitcast.76, bf16[512,1024,1]{1,0,2:T(8,128)(2,1)S(1)} %bitcast.74), kind=kOutput, calls=%fused_computation.2 | convolution fusion | flops 1074266112 | bytes 4194304 | tf_op jit(solution)/shard_map/nd,tdc->tnc/dot_general | solution.py:335
  80.2 1.5 copy.27
  81.7 0.0 copy-start.3
  81.7 29.5 %shard_map.123 = bf16[32,64,256]{2,1,0:T(8,128)(2,1)S(1)} custom-call(bf16[32,64,256]{2,1,0:T(8,128)(2,1)S(1)} %bitcast.56), custom_call_target="tpu_custom_call" | custom-call | flops 8589934592 | bytes 4194304 | tf_op jit(solution)/shard_map/pallas_call | solution.py:272
  111.2 0.1 bitcast_reduce_fusion
  111.3 2.5 %shard_map.124 = (bf16[256,256]{1,0:T(8,128)(2,1)}, bf16[256,256]{1,0:T(8,128)(2,1)}, f32[6,256]{1,0:T(8,128)S(1)}) custom-call(bf16[256,256]{1,0:T(8,128)(2,1)S(1)} %bitcast.62, bf16[256,256]{1,0:T(8,128)(2,1)S(1)} %bitcast.65, bf16[256,256]{1,0:T(8,128)(2,1)S(1)} %bitcast.68, f32[8,256]{1,0:T(8,128)S(1)} %pad_maximum_fusion.gate_ref, ...), custom_call_target="tpu_custom_call" | custom-call | flops 4294967296 | bytes 2097152 | tf_op jit(solution)/shard_map/pallas_call | solution.py:342
  113.8 0.1 reduce_sum.31
  114.0 0.1 slice_bitcast_fusion.1
  114.0 6.8 %shard_map.125 = f32[8,8,128]{2,1,0:T(8,128)S(1)} custom-call(f32[1,8,128]{2,1,0:T(8,128)S(1)} %fusion.1.src_ref), custom_call_target="tpu_custom_call" | custom-call | flops 8589934592 | bytes 4194304 | tf_op jit(solution)/shard_map/pallas_call | solution.py:272
  120.8 0.6 slice_reduce_fusion
  121.4 0.6 reshape.61
  122.0 2.9 %bitcast_convert_fusion.src_ref = bf16[8,64,1024]{2,1,0:T(8,128)(2,1)S(1)} fusion(bf16[4,8,64,256]{3,2,1,0:T(8,128)(2,1)S(1)} %bitcast.70, bf16[4,1024,256,1]{2,1,3,0:T(8,128)(2,1)} %bitcast.77), kind=kOutput, calls=%fused_computation | convolution fusion | flops 1074266112 | bytes 4194304 | tf_op jit(solution)/shard_map/tnlc,tdc->nld/dot_general | solution.py:334
  124.9 15.1 %shard_map.122 = bf16[8,64,1024]{2,1,0:T(8,128)(2,1)S(1)} custom-call(bf16[8,64,1024]{2,1,0:T(8,128)(2,1)S(1)} %bitcast_convert_fusion.src_ref), custom_call_target="tpu_custom_call" | custom-call | flops 8589934592 | bytes 4194304 | tf_op jit(solution)/shard_map/pallas_call | solution.py:272
  140.0 0.6 copy.24
  140.6 1.3 reshape.57
  (10 shorter events, 0.0 us)
Async XLA Ops:
  7.2 69.2 %all-gather.4.cloned.1.call-start = ((), (), s32[]{:S(2)}) async-start(), calls=%async_computation.1 | async-start | bytes 2621440 | tf_op jit(solution)/shard_map/all_gather | solution.py:300
  9.7 6.0 %copy-start.5 = (f32[2,2]{1,0:T(2,128)S(1)}, f32[2,2]{1,0:T(2,128)}, u32[]{:S(2)}) copy-start(f32[2,2]{1,0:T(2,128)} %param.14) | copy-start | bytes 52
  9.7 6.0 %copy-start.4 = (f32[2,1,2,256]{3,2,1,0:T(2,128)S(1)}, f32[2,1,2,256]{3,2,1,0:T(2,128)}, u32[]{:S(2)}) copy-start(f32[2,1,2,256]{3,2,1,0:T(2,128)} %param.13) | copy-start | bytes 12292
  9.7 6.1 %copy-start = (bf16[1,256,256]{2,1,0:T(8,128)(2,1)S(1)}, bf16[1,256,256]{2,1,0:T(8,128)(2,1)}, u32[]{:S(2)}) copy-start(bf16[1,256,256]{2,1,0:T(8,128)(2,1)} %param.10) | copy-start | bytes 393220
  9.8 6.1 %copy-start.1 = (bf16[1,256,256]{2,1,0:T(8,128)(2,1)S(1)}, bf16[1,256,256]{2,1,0:T(8,128)(2,1)}, u32[]{:S(2)}) copy-start(bf16[1,256,256]{2,1,0:T(8,128)(2,1)} %param.11) | copy-start | bytes 393220
  9.8 6.1 %copy-start.2 = (bf16[1,256,256]{2,1,0:T(8,128)(2,1)S(1)}, bf16[1,256,256]{2,1,0:T(8,128)(2,1)}, u32[]{:S(2)}) copy-start(bf16[1,256,256]{2,1,0:T(8,128)(2,1)} %param.12) | copy-start | bytes 393220
  11.3 65.0 %all-to-all-start = ((bf16[64,8,1024]{2,0,1:T(8,128)(2,1)}), bf16[64,8,1024]{2,0,1:T(8,128)(2,1)S(1)}, u32[]{:S(2)}, u32[]{:S(2)}) async-start(bf16[64,8,1024]{2,0,1:T(8,128)(2,1)} %copy.25), calls=%async_computation | async-start | bytes 2097152 | tf_op jit(solution)/shard_map/all_to_all | solution.py:301
  81.7 29.6 %copy-start.3 = (f32[1,1,2,128,128]{4,3,2,1,0:T(8,128)S(1)}, f32[1,1,2,128,128]{4,3,2,1,0:T(8,128)}, u32[]{:S(2)}) copy-start(f32[1,1,2,128,128]{4,3,2,1,0:T(8,128)} %param.15) | copy-start | bytes 393220
Sparse Core Ops, SparseCore 0:
  9.5 61.7 all-gather.3
